TPU v7x, 32 devices: a whole 2x2x4 slice. The times are simulated.
32 devices in a mesh: dp: 2 (over x), ha: 4 (over y, core), wa: 4 (over z).
Axes of the slice: x: 2, y: 2, z: 4, core: 2. Of those that a mesh axis runs over, the one named last changes fastest.
Arguments:
- queries: bfloat16 [2, 1, 4, 4, 144, 768], P('dp', None, 'ha', 'wa'), may hold values from -5 to 5
- key_tiles: bfloat16 [2, 1, 4, 4, 144, 768], P('dp', None, 'ha', 'wa'), may hold values from -5 to 5
- value_tiles: bfloat16 [2, 1, 4, 4, 144, 768], P('dp', None, 'ha', 'wa'), may hold values from -6 to 6
- out_grad: bfloat16 [2, 1, 4, 4, 144, 1536], P('dp', None, 'ha', 'wa'), may hold values from -8 to 8
- w_out: bfloat16 [1536, 768], replicated, may hold values from -0.21875 to 0.21875
- reaches: int32 [6, 6], replicated, may hold values from 0 to 1, as said below
Outputs:
- grad_query: bfloat16 [2, 1, 4, 4, 144, 768], P('dp', None, 'ha', 'wa')
- grad_key: bfloat16 [2, 1, 4, 4, 144, 768], P('dp', None, 'ha', 'wa')
- grad_value: bfloat16 [2, 1, 4, 4, 144, 768], P('dp', None, 'ha', 'wa')
- grad_w_out: float32 [1536, 768], P(('dp', 'ha', 'wa'))
Inputs may be any that keep to these rules, and one draw needn't show every extreme that they name: `reaches`: some head has every entry 1, and some other head has every entry 0.
All inputs are finite; a program needn't handle non-finite values.
Results may differ from a plain program's by a relative error of at most 0.018.
Values may be sent and summed in bfloat16 or wider, within the bound.
A program may use at most 128 MiB of HBM per device.

v0:
```python
import math

import jax
import jax.numpy as jnp
from jax import lax
from jax.sharding import PartitionSpec as P

HEADS = 6
HD = 128


def shifted(block, axis, distance):
    devices = range(lax.axis_size(axis))
    route = [(i - distance, i) for i in devices if i - distance in devices]
    return lax.ppermute(block, axis, route)


def padded_2(array, sides, width):
    for axis, dim in sides:
        size, length = (lax.axis_size(axis), array.shape[dim])
        up = [(i, (i + 1) % size) for i in range(size - 1)]
        down = [(j, i) for i, j in up]
        last = lax.slice_in_dim(array, length - width, length, axis=dim)
        initial = lax.slice_in_dim(array, 0, width, axis=dim)
        before = lax.ppermute(last, axis, up)
        after = lax.ppermute(initial, axis, down)
        array = jnp.concatenate([before, array, after], axis=dim)
    return array


def tile_allowed(reach_row, t_count, row_base, col_base, row_total, col_total):
    time_ids = jnp.arange(t_count)
    t_delta = time_ids[None, :] - time_ids[:, None]
    time_ok = (t_delta >= -reach_row[0]) & (t_delta <= reach_row[1])
    offsets = jnp.arange(3) - 1
    row_ok = (
        (offsets >= -reach_row[2])
        & (offsets <= reach_row[3])
        & (row_base + offsets >= 0)
        & (row_base + offsets < row_total)
    )
    col_ok = (
        (offsets >= -reach_row[4])
        & (offsets <= reach_row[5])
        & (col_base + offsets >= 0)
        & (col_base + offsets < col_total)
    )
    return time_ok[:, :, None, None] & row_ok[None, None, :, None] & col_ok[None, None, None, :]


def pass_along_width(edge_piece, offset):
    return shifted(edge_piece, "wa", offset)


def pass_along_height(edge_piece, offset):
    return shifted(edge_piece, "ha", offset)


def shards(queries, key_tiles, value_tiles, out_grad, w_out, reaches):
    t_count = queries.shape[1]
    tile_len = queries.shape[4]
    width_q = queries.shape[5]
    model_width = out_grad.shape[5]
    token_rows = t_count * tile_len
    key_count = t_count * 9 * tile_len
    softmax_scale = 1.0 / math.sqrt(HD)
    row_base = lax.axis_index("ha")
    col_base = lax.axis_index("wa")
    row_total = lax.axis_size("ha")
    col_total = lax.axis_size("wa")
    key_value = jnp.concatenate([key_tiles, value_tiles], axis=5)
    padded = padded_2(key_value, (("ha", 2), ("wa", 3)), 1)
    padded = padded.reshape(key_count, 2 * width_q)
    query_rows = queries.reshape(token_rows, width_q)
    grad_rows = out_grad.reshape(token_rows, model_width)
    grad_attn = jnp.dot(grad_rows, w_out, preferred_element_type=jnp.float32).astype(jnp.bfloat16)
    attn_list, gq_list, gk_list, gv_list = ([], [], [], [])
    for head_index in range(HEADS):
        col_start = head_index * HD
        col_stop = col_start + HD
        query_head = query_rows[:, col_start:col_stop]
        key_head = padded[:, col_start:col_stop]
        value_head = padded[:, width_q + col_start : width_q + col_stop]
        grad_head = grad_attn[:, col_start:col_stop]
        tile_pairs = tile_allowed(
            reaches[head_index], t_count, row_base, col_base, row_total, col_total
        )
        allowed = jnp.broadcast_to(
            tile_pairs[:, None, :, :, :, None], (t_count, tile_len, t_count, 3, 3, tile_len)
        ).reshape(token_rows, key_count)
        scores = (
            jnp.einsum("ad,bd->ab", query_head, key_head, preferred_element_type=jnp.float32)
            * softmax_scale
        )
        masked = jnp.where(allowed, scores, -jnp.inf)
        row_peak = jnp.max(masked, axis=1, keepdims=True)
        exp_terms = jnp.exp(masked - row_peak)
        prob_rows = exp_terms / jnp.sum(exp_terms, axis=1, keepdims=True)
        probs_low = prob_rows.astype(jnp.bfloat16)
        attn_head = jnp.dot(probs_low, value_head, preferred_element_type=jnp.float32).astype(
            jnp.bfloat16
        )
        row_delta = jnp.sum(
            grad_head.astype(jnp.float32) * attn_head.astype(jnp.float32), axis=1, keepdims=True
        )
        grad_probs = jnp.einsum(
            "ad,bd->ab", grad_head, value_head, preferred_element_type=jnp.float32
        )
        grad_scores = (prob_rows * (grad_probs - row_delta)).astype(jnp.bfloat16)
        grad_q_head = (
            jnp.dot(grad_scores, key_head, preferred_element_type=jnp.float32) * softmax_scale
        ).astype(jnp.bfloat16)
        grad_k_head = (
            jnp.einsum("ab,ad->bd", grad_scores, query_head, preferred_element_type=jnp.float32)
            * softmax_scale
        )
        grad_v_head = jnp.einsum(
            "ab,ad->bd", probs_low, grad_head, preferred_element_type=jnp.float32
        )
        attn_list.append(attn_head)
        gq_list.append(grad_q_head)
        gk_list.append(grad_k_head)
        gv_list.append(grad_v_head)
    attended = jnp.concatenate(attn_list, axis=1)
    grad_query = jnp.concatenate(gq_list, axis=1).reshape(queries.shape)
    partial_value = jnp.concatenate(gk_list + gv_list, axis=1).reshape(
        t_count, 3, 3, tile_len, 2 * width_q
    )
    from_right = pass_along_width(partial_value[:, :, 0], -1)
    from_left = pass_along_width(partial_value[:, :, 2], 1)
    middle = partial_value[:, :, 1] + from_right + from_left
    summed = middle[:, 1] + pass_along_height(middle[:, 0], -1) + pass_along_height(middle[:, 2], 1)
    grad_key = summed[:, :, :width_q].astype(jnp.bfloat16).reshape(queries.shape)
    grad_value = summed[:, :, width_q:].astype(jnp.bfloat16).reshape(queries.shape)
    grad_w_out = lax.psum_scatter(
        lax.dot_general(
            grad_rows, attended, (((0,), (0,)), ((), ())), preferred_element_type=jnp.float32
        ),
        ("dp", "ha", "wa"),
        scatter_dimension=0,
        tiled=True,
    )
    return (grad_query, grad_key, grad_value, grad_w_out)


def solution(mesh):
    in_specs = (
        P("dp", None, "ha", "wa", None, None),
        P("dp", None, "ha", "wa", None, None),
        P("dp", None, "ha", "wa", None, None),
        P("dp", None, "ha", "wa", None, None),
        P(),
        P(),
    )
    out_specs = (
        P("dp", None, "ha", "wa", None, None),
        P("dp", None, "ha", "wa", None, None),
        P("dp", None, "ha", "wa", None, None),
        P(("dp", "ha", "wa"), None),
    )
    return jax.shard_map(shards, mesh=mesh, in_specs=in_specs, out_specs=out_specs, check_vma=False)
```

profile of v0, /device:TPU:0, one launch (start us, length us, event | category | flops | bytes accessed | tf_op | source)
XLA Modules:
  0.0 227.1 jit_solution(10802643429050044560)
XLA Ops:
  9.3 1.3 collective-permute-start.1
  10.6 3.8 %collective-permute-start = (bf16[1,1,1,1,144,1536]{5,4,3,2,1,0:T(8,128)(2,1)S(1)}, bf16[1,1,1,1,144,1536]{5,4,3,2,1,0:T(8,128)(2,1)}, u32[]{:S(2)}, u32[]{:S(2)}) collective-permute-start(bf16[1,1,1,1,144,1536]{5,4,3,2,1,0:T(8,128)(2,1)S(1)} %constant_dynamic-update-slice_fusion), channel_id=1, source_target_pairs={{0,4},{4,8},{8,12},{1,5},{5,9},{9,13},{2,6},{6,10},{10,14},{3,7},{... | collective-permute-start | bytes 1327112 | tf_op jit(solution)/shard_map/ppermute | solution.py:25
  14.4 2.0 fusion.122
  21.4 1.3 and_and_fusion.8
  27.0 2.1 fusion.121
  39.2 2.4 %pad_maximum_fusion.1 = bf16[1,1,3,1,144,1536]{5,4,3,2,1,0:T(8,128)(2,1)} fusion(bf16[1,1,1,1,144,1536]{5,4,3,2,1,0:T(8,128)(2,1)} %collective-permute-done.1, bf16[1,1,1,1,144,1536]{5,4,3,2,1,0:T(8,128)(2,1)S(1)} %constant_dynamic-update-slice_fusion, bf16[1,1,1,1,144,1536]{5,4,3,2,1,0:T(8,128)(2,1)} %collective-permute-done), kind=kLoop, calls=%fused_computation.55 | loop fusion | flops 1327104 | bytes 2654208 | tf_op jit(solution)/shard_map/concatenate | solution.py:27
  41.5 1.3 collective-permute-start.3
  42.8 6.7 %collective-permute-start.2 = (bf16[1,1,3,1,144,1536]{5,4,3,2,1,0:T(8,128)(2,1)}, bf16[1,1,3,1,144,1536]{5,4,3,2,1,0:T(8,128)(2,1)}, u32[]{:S(2)}, u32[]{:S(2)}) collective-permute-start(bf16[1,1,3,1,144,1536]{5,4,3,2,1,0:T(8,128)(2,1)} %pad_maximum_fusion.1), channel_id=1, source_target_pairs={{0,1},{1,2},{2,3},{4,5},{5,6},{6,7},{8,9},{9,10},{10,11},{12,13},{... | collective-permute-start | bytes 3981320 | tf_op jit(solution)/shard_map/ppermute | solution.py:25
  51.2 1.3 and_and_fusion.5
  53.6 22.9 %collective-permute-done.3 = bf16[1,1,3,1,144,1536]{5,4,3,2,1,0:T(8,128)(2,1)} collective-permute-done((bf16[1,1,3,1,144,1536]{5,4,3,2,1,0:T(8,128)(2,1)}, bf16[1,1,3,1,144,1536]{5,4,3,2,1,0:T(8,128)(2,1)}, u32[]{:S(2)}, u32[]{:S(2)}) %collective-permute-start.3) | collective-permute-done | bytes 1327136 | tf_op jit(solution)/shard_map/ppermute | solution.py:26
  77.8 2.2 pad_maximum_fusion
  92.1 3.0 %convolution_bitcast_fusion = f32[1536,768]{0,1:T(8,128)} fusion(bf16[144,768]{1,0:T(8,128)(2,1)S(1)} %constant_dynamic-update-slice_fusion.2, bf16[1,1,1,1,144,1536]{5,4,3,2,1,0:T(8,128)(2,1)S(1)} %copy-done.3), kind=kOutput, calls=%fused_computation.1 | convolution fusion | flops 339738624 | bytes 5382144 | tf_op jit(solution)/shard_map/dot_general | solution.py:136
  95.1 6.1 %copy.18 = f32[1536,768]{1,0:T(8,128)} copy(f32[1536,768]{0,1:T(8,128)} %convolution_bitcast_fusion) | data formatting | bytes 9437184
  101.2 1.5 fusion.19
  102.7 1.4 fusion.18
  104.1 1.5 fusion.17
  105.6 1.4 fusion.16
  111.7 1.6 collective-permute-start.4
  113.3 5.2 %collective-permute-start.5 = (f32[1,3,144,1536]{3,2,1,0:T(8,128)S(1)}, f32[1,3,144,1536]{3,2,1,0:T(8,128)S(1)}, u32[]{:S(2)}, u32[]{:S(2)}) collective-permute-start(f32[1,3,144,1536]{3,2,1,0:T(8,128)S(1)} %get-tuple-element.19), channel_id=1, source_target_pairs={{0,1},{1,2},{2,3},{4,5},{5,6},{6,7},{8,9},{9,10},{10,11},{12,13},{... | collective-permute-start | bytes 7962632 | tf_op jit(solution)/shard_map/ppermute | solution.py:15
  119.0 67.4 %collective-permute-done.4 = f32[1,3,144,1536]{3,2,1,0:T(8,128)S(1)} collective-permute-done((f32[1,3,144,1536]{3,2,1,0:T(8,128)S(1)}, f32[1,3,144,1536]{3,2,1,0:T(8,128)S(1)}, u32[]{:S(2)}, u32[]{:S(2)}) %collective-permute-start.4) | collective-permute-done | bytes 2654240 | tf_op jit(solution)/shard_map/ppermute | solution.py:15
  186.4 3.3 %collective-permute-done.5 = f32[1,3,144,1536]{3,2,1,0:T(8,128)S(1)} collective-permute-done((f32[1,3,144,1536]{3,2,1,0:T(8,128)S(1)}, f32[1,3,144,1536]{3,2,1,0:T(8,128)S(1)}, u32[]{:S(2)}, u32[]{:S(2)}) %collective-permute-start.5) | collective-permute-done | bytes 2654240 | tf_op jit(solution)/shard_map/ppermute | solution.py:15
  190.7 1.3 collective-permute-start.6
  192.0 3.1 %collective-permute-start.7 = (f32[1,144,1536]{2,1,0:T(8,128)S(1)}, f32[1,144,1536]{2,1,0:T(8,128)S(1)}, u32[]{:S(2)}, u32[]{:S(2)}) collective-permute-start(f32[1,144,1536]{2,1,0:T(8,128)S(1)} %get-tuple-element.21), channel_id=1, source_target_pairs={{0,4},{4,8},{8,12},{1,5},{5,9},{9,13},{2,6},{6,10},{10,14},{3,7},{... | collective-permute-start | bytes 2654216 | tf_op jit(solution)/shard_map/ppermute | solution.py:15
  198.0 22.2 %reduce-scatter.4.cloned.1.call-done = f32[48,768]{1,0:T(8,128)} async-done(((f32[1536,768]{1,0:T(8,128)}), f32[48,768]{1,0:T(8,128)}) %reduce-scatter.4.cloned.1.call-update) | async-done | bytes 147472
  (126 shorter events, 31.3 us)
Async XLA Ops:
  7.2 45.9 %copy-start = (bf16[1536,768]{1,0:T(8,128)(2,1)S(1)}, bf16[1536,768]{1,0:T(8,128)(2,1)}, u32[]{:S(2)}) copy-start(bf16[1536,768]{1,0:T(8,128)(2,1)} %param.10) | copy-start | bytes 7077892
  7.2 45.9 %copy-start.3 = (bf16[1,1,1,1,144,1536]{5,4,3,2,1,0:T(8,128)(2,1)S(1)}, bf16[1,1,1,1,144,1536]{5,4,3,2,1,0:T(8,128)(2,1)}, u32[]{:S(2)}) copy-start(bf16[1,1,1,1,144,1536]{5,4,3,2,1,0:T(8,128)(2,1)} %param.9) | copy-start | bytes 1327108
  7.2 213.0 %reduce-scatter.4.cloned.1.call-start = ((), (), s32[]{:S(2)}) async-start(), calls=%async_computation.1 | async-start | bytes 4866048
  9.3 29.8 %collective-permute-start.1 = (bf16[1,1,1,1,144,1536]{5,4,3,2,1,0:T(8,128)(2,1)S(1)}, bf16[1,1,1,1,144,1536]{5,4,3,2,1,0:T(8,128)(2,1)}, u32[]{:S(2)}, u32[]{:S(2)}) collective-permute-start(bf16[1,1,1,1,144,1536]{5,4,3,2,1,0:T(8,128)(2,1)S(1)} %constant_dynamic-update-slice_fusion), channel_id=1, source_target_pairs={{4,0},{8,4},{12,8},{5,1},{9,5},{13,9},{6,2},{10,6},{14,10},{7,3},{... | collective-permute-start | bytes 1327112 | tf_op jit(solution)/shard_map/ppermute | solution.py:26
  10.6 28.6 %collective-permute-start = (bf16[1,1,1,1,144,1536]{5,4,3,2,1,0:T(8,128)(2,1)S(1)}, bf16[1,1,1,1,144,1536]{5,4,3,2,1,0:T(8,128)(2,1)}, u32[]{:S(2)}, u32[]{:S(2)}) collective-permute-start(bf16[1,1,1,1,144,1536]{5,4,3,2,1,0:T(8,128)(2,1)S(1)} %constant_dynamic-update-slice_fusion), channel_id=1, source_target_pairs={{0,4},{4,8},{8,12},{1,5},{5,9},{9,13},{2,6},{6,10},{10,14},{3,7},{... | collective-permute-start | bytes 1327112 | tf_op jit(solution)/shard_map/ppermute | solution.py:25
  41.5 35.1 %collective-permute-start.3 = (bf16[1,1,3,1,144,1536]{5,4,3,2,1,0:T(8,128)(2,1)}, bf16[1,1,3,1,144,1536]{5,4,3,2,1,0:T(8,128)(2,1)}, u32[]{:S(2)}, u32[]{:S(2)}) collective-permute-start(bf16[1,1,3,1,144,1536]{5,4,3,2,1,0:T(8,128)(2,1)} %pad_maximum_fusion.1), channel_id=1, source_target_pairs={{1,0},{2,1},{3,2},{5,4},{6,5},{7,6},{9,8},{10,9},{11,10},{13,12},{... | collective-permute-start | bytes 3981320 | tf_op jit(solution)/shard_map/ppermute | solution.py:26
  42.8 35.0 %collective-permute-start.2 = (bf16[1,1,3,1,144,1536]{5,4,3,2,1,0:T(8,128)(2,1)}, bf16[1,1,3,1,144,1536]{5,4,3,2,1,0:T(8,128)(2,1)}, u32[]{:S(2)}, u32[]{:S(2)}) collective-permute-start(bf16[1,1,3,1,144,1536]{5,4,3,2,1,0:T(8,128)(2,1)} %pad_maximum_fusion.1), channel_id=1, source_target_pairs={{0,1},{1,2},{2,3},{4,5},{5,6},{6,7},{8,9},{9,10},{10,11},{12,13},{... | collective-permute-start | bytes 3981320 | tf_op jit(solution)/shard_map/ppermute | solution.py:25
  53.6 37.4 %copy-start.22 = (bf16[144,768]{1,0:T(8,128)(2,1)}, bf16[144,768]{1,0:T(8,128)(2,1)S(1)}, u32[]{:S(2)}) copy-start(bf16[144,768]{1,0:T(8,128)(2,1)S(1)} %convolution_convert_fusion) | copy-start | bytes 663556
  53.6 26.4 %copy-start.21 = (bf16[1,1,1,1,144,768]{5,4,3,2,1,0:T(8,128)(2,1)S(1)}, bf16[1,1,1,1,144,768]{5,4,3,2,1,0:T(8,128)(2,1)}, u32[]{:S(2)}) copy-start(bf16[1,1,1,1,144,768]{5,4,3,2,1,0:T(8,128)(2,1)} %param.6) | copy-start | bytes 663556
  80.0 11.0 %copy-start.1 = (bf16[1,1,3,3,144,1536]{5,4,3,2,1,0:T(8,128)(2,1)}, bf16[1,1,3,3,144,1536]{5,4,3,2,1,0:T(8,128)(2,1)S(1)}, u32[]{:S(2)}) copy-start(bf16[1,1,3,3,144,1536]{5,4,3,2,1,0:T(8,128)(2,1)S(1)} %pad_maximum_fusion) | copy-start | bytes 11943940
  81.6 7.2 %copy-start.10 = (f32[1296,144]{0,1:T(8,128)}, f32[1296,144]{0,1:T(8,128)S(1)}, u32[]{:S(2)}) copy-start(f32[1296,144]{0,1:T(8,128)S(1)} %get-tuple-element.67) | copy-start | bytes 2239492
  82.0 7.9 %copy-start.12 = (f32[1296,144]{0,1:T(8,128)}, f32[1296,144]{0,1:T(8,128)S(1)}, u32[]{:S(2)}) copy-start(f32[1296,144]{0,1:T(8,128)S(1)} %get-tuple-element.65) | copy-start | bytes 2239492
  82.4 8.6 %copy-start.14 = (f32[1296,144]{0,1:T(8,128)}, f32[1296,144]{0,1:T(8,128)S(1)}, u32[]{:S(2)}) copy-start(f32[1296,144]{0,1:T(8,128)S(1)} %get-tuple-element.63) | copy-start | bytes 2239492
  101.2 6.6 %copy-start.15 = (f32[1296,144]{0,1:T(8,128)S(1)}, f32[1296,144]{0,1:T(8,128)}, u32[]{:S(2)}) copy-start(f32[1296,144]{0,1:T(8,128)} %copy-done.14) | copy-start | bytes 2239492
  101.2 6.6 %copy-start.23 = (bf16[144,768]{1,0:T(8,128)(2,1)S(1)}, bf16[144,768]{1,0:T(8,128)(2,1)}, u32[]{:S(2)}) copy-start(bf16[144,768]{1,0:T(8,128)(2,1)} %copy-done.22) | copy-start | bytes 663556
  111.2 7.2 %copy-start.2 = (bf16[1,1,3,3,144,1536]{5,4,3,2,1,0:T(8,128)(2,1)S(1)}, bf16[1,1,3,3,144,1536]{5,4,3,2,1,0:T(8,128)(2,1)}, u32[]{:S(2)}) copy-start(bf16[1,1,3,3,144,1536]{5,4,3,2,1,0:T(8,128)(2,1)} %copy-done.1) | copy-start | bytes 11943940
  111.2 7.2 %copy-start.20 = (bf16[144,1296]{1,0:T(8,128)(2,1)S(1)}, bf16[144,1296]{1,0:T(8,128)(2,1)}, u32[]{:S(2)}) copy-start(bf16[144,1296]{1,0:T(8,128)(2,1)} %fusion.20) | copy-start | bytes 1119748
  111.2 7.5 %copy-start.19 = (bf16[144,1296]{1,0:T(8,128)(2,1)S(1)}, bf16[144,1296]{1,0:T(8,128)(2,1)}, u32[]{:S(2)}) copy-start(bf16[144,1296]{1,0:T(8,128)(2,1)} %fusion.21) | copy-start | bytes 1119748
  111.7 74.7 %collective-permute-start.4 = (f32[1,3,144,1536]{3,2,1,0:T(8,128)S(1)}, f32[1,3,144,1536]{3,2,1,0:T(8,128)S(1)}, u32[]{:S(2)}, u32[]{:S(2)}) collective-permute-start(f32[1,3,144,1536]{3,2,1,0:T(8,128)S(1)} %get-tuple-element.18), channel_id=1, source_target_pairs={{1,0},{2,1},{3,2},{5,4},{6,5},{7,6},{9,8},{10,9},{11,10},{13,12},{... | collective-permute-start | bytes 7962632 | tf_op jit(solution)/shard_map/ppermute | solution.py:15
  113.3 76.4 %collective-permute-start.5 = (f32[1,3,144,1536]{3,2,1,0:T(8,128)S(1)}, f32[1,3,144,1536]{3,2,1,0:T(8,128)S(1)}, u32[]{:S(2)}, u32[]{:S(2)}) collective-permute-start(f32[1,3,144,1536]{3,2,1,0:T(8,128)S(1)} %get-tuple-element.19), channel_id=1, source_target_pairs={{0,1},{1,2},{2,3},{4,5},{5,6},{6,7},{8,9},{9,10},{10,11},{12,13},{... | collective-permute-start | bytes 7962632 | tf_op jit(solution)/shard_map/ppermute | solution.py:15
  119.0 76.1 %copy-start.18 = (bf16[144,1296]{1,0:T(8,128)(2,1)S(1)}, bf16[144,1296]{1,0:T(8,128)(2,1)}, u32[]{:S(2)}) copy-start(bf16[144,1296]{1,0:T(8,128)(2,1)} %fusion.22) | copy-start | bytes 1119748
  190.7 5.6 %collective-permute-start.6 = (f32[1,144,1536]{2,1,0:T(8,128)S(1)}, f32[1,144,1536]{2,1,0:T(8,128)S(1)}, u32[]{:S(2)}, u32[]{:S(2)}) collective-permute-start(f32[1,144,1536]{2,1,0:T(8,128)S(1)} %get-tuple-element.20), channel_id=1, source_target_pairs={{4,0},{8,4},{12,8},{5,1},{9,5},{13,9},{6,2},{10,6},{14,10},{7,3},{... | collective-permute-start | bytes 2654216 | tf_op jit(solution)/shard_map/ppermute | solution.py:15
  192.0 5.1 %collective-permute-start.7 = (f32[1,144,1536]{2,1,0:T(8,128)S(1)}, f32[1,144,1536]{2,1,0:T(8,128)S(1)}, u32[]{:S(2)}, u32[]{:S(2)}) collective-permute-start(f32[1,144,1536]{2,1,0:T(8,128)S(1)} %get-tuple-element.21), channel_id=1, source_target_pairs={{0,4},{4,8},{8,12},{1,5},{5,9},{9,13},{2,6},{6,10},{10,14},{3,7},{... | collective-permute-start | bytes 2654216 | tf_op jit(solution)/shard_map/ppermute | solution.py:15
  196.3 23.9 %copy-start.24 = (bf16[144,768]{1,0:T(8,128)(2,1)}, bf16[144,768]{1,0:T(8,128)(2,1)S(1)}, u32[]{:S(2)}) copy-start(bf16[144,768]{1,0:T(8,128)(2,1)S(1)} %fusion.37) | copy-start | bytes 663556
  (10 other events, 38.4 us)
Sparse Core Ops, SparseCore 0:
  101.3 118.8 reduce-scatter.3
where the time goes:
time: 228 us; the launch traced here: 227 us
  waiting for transfers between devices  118 us (52%)
  between operations  29.7 us (13%)
  matrix products  25.1 us (11%)
  starting transfers between devices  24.2 us (11%)
  local copies, waits for them, and re-layouts  15.2 us (7%)
  other arithmetic  15.2 us (7%)
    ppermute x4, waiting for transfers between devices, shifted(): return lax.ppermute(block, axis, route)  71.4 us
    ppermute x2, waiting for transfers between devices, padded_2(): after = lax.ppermute(initial, axis, down)  23 us
    unnamed x2, waiting for transfers between devices  22.2 us
    ppermute x4, starting transfers between devices, shifted(): return lax.ppermute(block, axis, route)  11.1 us
    ppermute x2, starting transfers between devices, padded_2(): before = lax.ppermute(last, axis, up)  10.5 us
    unnamed x52, local copies, waits for them, and re-layouts  7.7 us
    dot_general x6, matrix products, shards(): jnp.einsum('ab,ad->bd', grad_scores, query_head, preferred_element_type=j...  6.52 us
    dot_general x6, matrix products, shards(): jnp.einsum('ad,bd->ab', grad_head, value_head, preferred_element_type=jnp...  5.65 us
  transfers between devices with their start and end apart: 9, of which 6 were waited for; matrix products, arithmetic and copies ran while one was open for 12% of the time, Pallas kernels for 0%

commit v1 on v0

v1 whole, which is shorter than its diff:
```python
import functools
import math

import jax
import jax.numpy as jnp
from jax import lax
from jax.experimental import pallas as pl
from jax.experimental.pallas import tpu as pltpu
from jax.sharding import PartitionSpec as P

HD = 128
BF = jnp.bfloat16
F32 = jnp.float32
OUTSIDE = -1e30


def dot(a, b, dims):
    return lax.dot_general(a, b, (dims, ((), ())), preferred_element_type=F32)


def kernel(
    sizes, heads, q_ref, k_ref, v_ref, og_ref, w_ref, reach_ref, gq_ref, gk_ref, gv_ref, gw_ref,
    kv, q_sl, da_sl, og_s, og_g, og_t, att, s_ref, dp_ref, p_low, ds_low,
    back_out, back_in, side_out, side_in, acc, dk_sl, dq_sl, dw_out, dw_in, dw_sl,
    w_send, w_recv, h_send, h_recv, bh_send, bh_recv, bw_send, bw_recv,
    og_send, og_recv, at_send, at_recv, dw_send, dw_recv,
):
    n_dp, n_ha, n_wa = sizes
    sent = heads - 1
    tile = q_ref.shape[0]
    model = og_ref.shape[1]
    quarter = model // 4
    block = gw_ref.shape[0]
    run = n_wa * block
    scale = 1.0 / math.sqrt(HD)
    dp, ha, wa = (lax.axis_index(a) for a in ("dp", "ha", "wa"))
    dp_hi, dp_lo = dp // 2, dp % 2
    ha_hi, ha_lo = ha // 2, ha % 2
    wide = ((wa > 0, (dp, ha, wa - 1)), (wa < n_wa - 1, (dp, ha, wa + 1)))
    high = ((ha > 0, (dp, ha - 1, wa)), (ha < n_ha - 1, (dp, ha + 1, wa)))
    group = []
    for j in range(1, 4):
        d_lo = (1 - dp_lo) if j // 2 else dp_lo
        h_lo = (1 - ha_lo) if j % 2 else ha_lo
        group.append((d_lo * 2 + h_lo, (dp_hi * 2 + d_lo, ha_hi * 2 + h_lo, wa)))
    runs = (n_dp // 2) * (n_ha // 2)
    peers = runs * n_wa
    my_peer = (dp_hi * (n_ha // 2) + ha_hi) * n_wa + wa

    def peer_at(step):
        at = lax.rem(my_peer + step, peers)
        r = at // n_wa
        return at, (
            (r // (n_ha // 2)) * 2 + dp_lo,
            (r % (n_ha // 2)) * 2 + ha_lo,
            at % n_wa,
        )

    def remote(src, dst, s, r, device):
        return pltpu.make_async_remote_copy(
            src_ref=src, dst_ref=dst, send_sem=s, recv_sem=r, device_id=device,
            device_id_type=pl.DeviceIdType.MESH,
        )

    def w_copy(d, i):
        return remote(
            kv.at[i, 4], kv.at[i, 3 + 2 * (1 - d)], w_send.at[d, i], w_recv.at[d, i], wide[d][1]
        )

    def h_copy(d, c, i):
        return remote(
            kv.at[i, 3 + c], kv.at[i, 6 * (1 - d) + c], h_send.at[d, c, i], h_recv.at[d, c, i],
            high[d][1],
        )

    def bh_copy(d, i):
        return remote(
            back_out.at[i, d], back_in.at[i, d], bh_send.at[d, i], bh_recv.at[d, i], high[d][1]
        )

    def bw_copy(d, i):
        return remote(
            side_out.at[i, d], side_in.at[i, d], bw_send.at[d, i], bw_recv.at[d, i], wide[d][1]
        )

    def og_copy(j):
        member, device = group[j - 1]
        return remote(og_s.at[member], og_g.at[j], og_send.at[j - 1], og_recv.at[j - 1], device)

    def at_copy(j, i):
        return remote(
            att.at[i, 0], att.at[i, j], at_send.at[j - 1, i], at_recv.at[j - 1, i],
            group[j - 1][1],
        )

    def dw_copy(step, i):
        at, device = peer_at(step)
        return remote(
            dw_out.at[i, at], dw_in.at[i, step - 1], dw_send.at[step - 1, i],
            dw_recv.at[step - 1, i], device,
        )

    barrier = pltpu.get_barrier_semaphore()

    def greet(device):
        pl.semaphore_signal(
            barrier, inc=1, device_id=device, device_id_type=pl.DeviceIdType.MESH
        )

    for exists, device in wide + high:
        pl.when(exists)(functools.partial(greet, device))
    for _, device in group:
        greet(device)
    for step in range(1, peers):
        greet(peer_at(step)[1])

    alone = jnp.int32(0)
    for n in reversed(range(heads)):
        reach = reach_ref[n, 2] + reach_ref[n, 3] + reach_ref[n, 4] + reach_ref[n, 5]
        alone = jnp.where(reach == 0, n, alone)

    def pick(i, read):
        if i < sent:
            return jnp.where(alone <= i, read(i + 1), read(i))
        value = read(0)
        for n in range(1, heads):
            value = jnp.where(alone == n, read(n), value)
        return value

    def place(n, read):
        value = read(sent)
        if n < sent:
            value = jnp.where(alone > n, read(n), value)
        if n > 0:
            value = jnp.where(alone < n, read(n - 1), value)
        return value

    def columns(ref):
        return lambda n: ref[:, n * HD : (n + 1) * HD]

    for i in range(sent):
        kv[i, 4, :, :HD] = pick(i, columns(k_ref))
        kv[i, 4, :, HD:] = pick(i, columns(v_ref))
    for m in range(4):
        for r in range(runs):
            first = (r // (n_ha // 2) * 2 + m // 2) * n_ha + (r % (n_ha // 2)) * 2 + m % 2
            og_s[m, :, r * run : (r + 1) * run] = og_ref[:, first * run : (first + 1) * run]

    for d in range(2):
        @pl.when(jnp.logical_not(wide[d][0]))
        def _():
            for i in range(sent):
                kv[i, 3 + 2 * d] = jnp.zeros((tile, 2 * HD), BF)
                side_in[i, 1 - d] = jnp.zeros((tile, 2 * HD), BF)

        @pl.when(jnp.logical_not(high[d][0]))
        def _():
            for i in range(sent):
                kv[i, 6 * d : 6 * d + 3] = jnp.zeros((3, tile, 2 * HD), BF)
                back_in[i, 1 - d] = jnp.zeros((3, tile, 2 * HD), BF)

    waits = 3 + peers - 1
    for exists, _ in wide + high:
        waits = waits + jnp.where(exists, 1, 0)
    pl.semaphore_wait(barrier, waits)

    for i in range(sent):
        for d in range(2):
            @pl.when(wide[d][0])
            def _():
                w_copy(d, i).start()

            @pl.when(high[d][0])
            def _():
                h_copy(d, 1, i).start()
    for j in range(1, 4):
        og_copy(j).start()

    grad_attn = dot(og_ref[...], w_ref[...], ((1,), (0,))).astype(BF)
    for i in range(heads):
        q_sl[i] = pick(i, columns(q_ref))
        da_sl[i] = pick(i, columns(grad_attn))

    def attend(i, q, da, k, v, keys, bias):
        def rows(c):
            return slice(c * 16, (c + 1) * 16)

        s_ref[:, :keys] = dot(q, k, ((1,), (1,)))
        dp_ref[:, :keys] = dot(da, v, ((1,), (1,)))
        for c in range(tile // 16):
            s = s_ref[rows(c), :keys] * scale
            if bias is not None:
                s = s + bias
            e = jnp.exp(s - jnp.max(s, axis=1, keepdims=True))
            p = e * (1.0 / jnp.sum(e, axis=1, keepdims=True))
            s_ref[rows(c), :keys] = p
            p_low[rows(c), :keys] = p.astype(BF)
        attended = dot(p_low[:, :keys], v, ((1,), (0,))).astype(BF)
        att[i, 0] = attended
        delta = jnp.sum(da.astype(F32) * attended.astype(F32), axis=1, keepdims=True)
        for c in range(tile // 16):
            ds = s_ref[rows(c), :keys] * (dp_ref[rows(c), :keys] - delta[rows(c)])
            ds_low[rows(c), :keys] = ds.astype(BF)
        dq_sl[i] = (dot(ds_low[:, :keys], k, ((1,), (0,))) * scale).astype(BF)
        dk = dot(ds_low[:, :keys], q, ((0,), (0,))) * scale
        dv = dot(p_low[:, :keys], da, ((0,), (0,)))
        return dk, dv

    dk, dv = attend(
        sent, q_sl[sent], da_sl[sent], pick(sent, columns(k_ref)), pick(sent, columns(v_ref)), tile, None
    )
    dk_sl[sent, :, :HD] = dk.astype(BF)
    dk_sl[sent, :, HD:] = dv.astype(BF)
    for j in range(1, 4):
        at_copy(j, sent).start()

    def relay(i):
        for d in range(2):
            @pl.when(wide[1 - d][0])
            def _():
                w_copy(d, i).wait_recv()
        for d in range(2):
            @pl.when(high[d][0])
            def _():
                h_copy(d, 0, i).start()
                h_copy(d, 2, i).start()

    def fold_high(i):
        for d in range(2):
            @pl.when(high[1 - d][0])
            def _():
                bh_copy(d, i).wait_recv()
        for d in range(2):
            c = 2 * d
            side_out[i, d] = (
                acc[i, c] + back_in[i, 0, c].astype(F32) + back_in[i, 1, c].astype(F32)
            ).astype(BF)
        acc[i, 1] = acc[i, 1] + back_in[i, 0, 1].astype(F32) + back_in[i, 1, 1].astype(F32)
        for d in range(2):
            @pl.when(wide[d][0])
            def _():
                bw_copy(d, i).start()

    def fold_wide(i):
        for d in range(2):
            @pl.when(wide[1 - d][0])
            def _():
                bw_copy(d, i).wait_recv()
        dk_sl[i] = (
            acc[i, 1] + side_in[i, 0].astype(F32) + side_in[i, 1].astype(F32)
        ).astype(BF)

    def project(i):
        for j in range(1, 4):
            at_copy(j, i).wait_recv()
        part = dot(og_t[...], att[i].reshape(4 * tile, HD), ((1,), (0,)))
        for b in range(peers):
            dw_out[i, b] = part[b * block : (b + 1) * block].astype(BF)
        for b in range(1, peers):
            dw_copy(b, i).start()

    def window(i):
        def reach(c):
            return jnp.where(alone <= i, reach_ref[i + 1, c], reach_ref[i, c])

        tiles = lax.broadcasted_iota(jnp.int32, (1, 9 * tile), 1)
        bias = jnp.zeros((1, 9 * tile), F32)
        before = (jnp.where((ha > 0) & (reach(2) > 0), 1, 0), 1,
                  jnp.where((ha < n_ha - 1) & (reach(3) > 0), 1, 0))
        beside = (jnp.where((wa > 0) & (reach(4) > 0), 1, 0), 1,
                  jnp.where((wa < n_wa - 1) & (reach(5) > 0), 1, 0))
        for t in range(9):
            open_ = jnp.where(before[t // 3] * beside[t % 3] > 0, 0.0, OUTSIDE)
            inside = (tiles >= t * tile) & (tiles < (t + 1) * tile)
            bias = jnp.where(inside, open_, bias)
        return bias

    relay(0)
    relay(1)
    for j in range(1, 4):
        og_copy(j).wait_recv()
    og_g[0] = og_s[dp_lo * 2 + ha_lo]
    og_t[...] = og_g[...].reshape(4 * tile, quarter).T
    project(sent)

    def step(i, carry):
        pl.when(i + 2 < sent)(lambda: relay(i + 2))
        for d in range(2):
            @pl.when(high[1 - d][0])
            def _():
                for c in range(3):
                    h_copy(d, c, i).wait_recv()
        near = kv[i].reshape(9 * tile, 2 * HD)
        dk, dv = attend(
            i, q_sl[i], da_sl[i], near[:, :HD], near[:, HD:], 9 * tile, window(i)
        )
        for j in range(1, 4):
            at_copy(j, i).start()
        dk = dk.reshape(3, 3, tile, HD)
        dv = dv.reshape(3, 3, tile, HD)
        for d in range(2):
            back_out[i, d, :, :, :HD] = dk[2 * d].astype(BF)
            back_out[i, d, :, :, HD:] = dv[2 * d].astype(BF)

            @pl.when(high[d][0])
            def _():
                bh_copy(d, i).start()
        acc[i, :, :, :HD] = dk[1]
        acc[i, :, :, HD:] = dv[1]

        @pl.when(i >= 1)
        def _():
            project(i - 1)
            fold_high(i - 1)
        pl.when(i >= 2)(lambda: fold_wide(i - 2))
        return carry

    lax.fori_loop(0, sent, step, 0)
    project(sent - 1)
    fold_high(sent - 1)
    if sent > 1:
        fold_wide(sent - 2)

    for n in range(heads):
        gq_ref[:, n * HD : (n + 1) * HD] = place(n, lambda i: dq_sl[i])

    def gather_w(i, carry):
        total = dw_out[i, my_peer].astype(F32)
        for b in range(1, peers):
            dw_copy(b, i).wait_recv()
            total = total + dw_in[i, b - 1].astype(F32)
        dw_sl[i] = total
        return carry

    lax.fori_loop(0, heads, gather_w, 0)
    fold_wide(sent - 1)
    for n in range(heads):
        at = slice(n * HD, (n + 1) * HD)
        gk_ref[:, at] = place(n, lambda i: dk_sl[i, :, :HD])
        gv_ref[:, at] = place(n, lambda i: dk_sl[i, :, HD:])
        gw_ref[:, at] = place(n, lambda i: dw_sl[i])

    def drain(i, carry):
        for d in range(2):
            @pl.when(wide[d][0])
            def _():
                w_copy(d, i).wait_send()
                bw_copy(d, i).wait_send()

            @pl.when(high[d][0])
            def _():
                for c in range(3):
                    h_copy(d, c, i).wait_send()
                bh_copy(d, i).wait_send()
        return carry

    lax.fori_loop(0, sent, drain, 0)

    def drain_w(i, carry):
        for j in range(1, 4):
            at_copy(j, i).wait_send()
        for b in range(1, peers):
            dw_copy(b, i).wait_send()
        return carry

    lax.fori_loop(0, heads, drain_w, 0)
    for j in range(1, 4):
        og_copy(j).wait_send()


def shards(sizes, queries, key_tiles, value_tiles, out_grad, w_out, reaches):
    tile, width = queries.shape[4:]
    model = out_grad.shape[5]
    heads = width // HD
    sent = heads - 1
    devices = sizes[0] * sizes[1] * sizes[2]
    block = model // devices
    peers = devices // 4
    rows = [a.reshape(a.shape[-2:]) for a in (queries, key_tiles, value_tiles, out_grad)]
    sem = pltpu.SemaphoreType.DMA
    vmem = pl.BlockSpec(memory_space=pltpu.VMEM)
    grads = jax.ShapeDtypeStruct((tile, width), BF)
    out = pl.pallas_call(
        functools.partial(kernel, sizes, heads),
        out_shape=(grads, grads, grads, jax.ShapeDtypeStruct((block, width), F32)),
        in_specs=[vmem] * 5 + [pl.BlockSpec(memory_space=pltpu.SMEM)],
        out_specs=(vmem,) * 4,
        scratch_shapes=[
            pltpu.VMEM((sent, 9, tile, 2 * HD), BF),
            pltpu.VMEM((heads, tile, HD), BF),
            pltpu.VMEM((heads, tile, HD), BF),
            pltpu.VMEM((4, tile, model // 4), BF),
            pltpu.VMEM((4, tile, model // 4), BF),
            pltpu.VMEM((model // 4, 4 * tile), BF),
            pltpu.VMEM((heads, 4, tile, HD), BF),
            pltpu.VMEM((tile, 9 * tile), F32),
            pltpu.VMEM((tile, 9 * tile), F32),
            pltpu.VMEM((tile, 9 * tile), BF),
            pltpu.VMEM((tile, 9 * tile), BF),
            pltpu.VMEM((sent, 2, 3, tile, 2 * HD), BF),
            pltpu.VMEM((sent, 2, 3, tile, 2 * HD), BF),
            pltpu.VMEM((sent, 2, tile, 2 * HD), BF),
            pltpu.VMEM((sent, 2, tile, 2 * HD), BF),
            pltpu.VMEM((sent, 3, tile, 2 * HD), F32),
            pltpu.VMEM((heads, tile, 2 * HD), BF),
            pltpu.VMEM((heads, tile, HD), BF),
            pltpu.VMEM((heads, peers, block, HD), BF),
            pltpu.VMEM((heads, peers - 1, block, HD), BF),
            pltpu.VMEM((heads, block, HD), F32),
            sem((2, sent)), sem((2, sent)), sem((2, 3, sent)), sem((2, 3, sent)),
            sem((2, sent)), sem((2, sent)), sem((2, sent)), sem((2, sent)),
            sem((3,)), sem((3,)), sem((3, heads)), sem((3, heads)),
            sem((peers - 1, heads)), sem((peers - 1, heads)),
        ],
        compiler_params=pltpu.CompilerParams(
            collective_id=0, has_side_effects=True, vmem_limit_bytes=60 * 1024 * 1024
        ),
    )(*rows, w_out, reaches)
    return tuple(o.reshape(queries.shape) for o in out[:3]) + (out[3],)


def solution(mesh):
    tiles = P("dp", None, "ha", "wa", None, None)
    sizes = tuple(mesh.shape[a] for a in ("dp", "ha", "wa"))
    return jax.shard_map(
        functools.partial(shards, sizes),
        mesh=mesh,
        in_specs=(tiles, tiles, tiles, tiles, P(), P()),
        out_specs=(tiles, tiles, tiles, P(("dp", "ha", "wa"), None)),
        check_vma=False,
    )
```

time: 228 us -> 54.2 us (0.24)
  waiting for transfers between devices: 118 us -> 0 us
  Pallas kernels: 0 us -> 46.5 us
  between operations: 29.7 us -> 0.64 us
  matrix products: 25.1 us -> 0 us
  starting transfers between devices: 24.2 us -> 0 us
  other arithmetic: 15.2 us -> 0 us
  local copies, waits for them, and re-layouts: 15.2 us -> 6.48 us
    ppermute x8 -> x0, waiting for transfers between devices: 95.5 us -> none  [the longest x4 71.4 us: shifted(): return lax.ppermute(block, axis, route)]
    pallas_call x0 -> x1, Pallas kernels: none -> 46.5 us  [shards(): pl.pallas_call(functools.partial(kernel, sizes, heads), out_shape=(grads,...]
    dot_general x38 -> x0, matrix products: 25.1 us -> none  [the longest x6 6.52 us: shards(): jnp.einsum('ab,ad->bd', grad_scores, query_head, preferred_element_type=j...]
    ppermute x8 -> x0, starting transfers between devices: 24.1 us -> none  [the longest x4 11.1 us: shifted(): return lax.ppermute(block, axis, route)]
    unnamed x2 -> x0, waiting for transfers between devices: 22.2 us -> none
    and x12 -> x0, other arithmetic: 8.02 us -> none  [the longest x9 4.22 us: tile_allowed(): time_ok[:, :, None, None] & row_ok[None, None, :, None]]
    concatenate x2 -> x0, other arithmetic: 4.56 us -> none  [padded_2(): array = jnp.concatenate([before, array, after], axis=dim)]
    slice x2 -> x0, local copies, waits for them, and re-layouts: 4.1 us -> none  [tile_allowed(): reach_row[2]]
  transfers between devices with their start and end apart: 9 -> 0, of which waited for: 6 -> 0; matrix products, arithmetic and copies ran while one was open for 12% -> 0% of each run, Pallas kernels for 0% -> 0%
where the time goes in v1:
time: 54.2 us; the launch traced here: 53.6 us
  Pallas kernels  46.5 us (86%)
  local copies, waits for them, and re-layouts  6.48 us (12%)
  between operations  0.64 us (1%)
    pallas_call x1, Pallas kernels, shards(): pl.pallas_call(functools.partial(kernel, sizes, heads), out_shape=(grads,...  46.5 us
    unnamed x4, local copies, waits for them, and re-layouts  6.48 us

profile of v1, /device:TPU:0, one launch (start us, length us, event | category | flops | bytes accessed | tf_op | source)
XLA Modules:
  0.0 53.6 jit_solution(15460612778112750210)
XLA Ops:
  0.6 46.5 %shard_map.93 = (bf16[144,768]{1,0:T(8,128)(2,1)}, bf16[144,768]{1,0:T(8,128)(2,1)}, bf16[144,768]{1,0:T(8,128)(2,1)}, f32[48,768]{1,0:T(8,128)}) custom-call(bf16[144,768]{1,0:T(8,128)(2,1)} %bitcast.11, bf16[144,768]{1,0:T(8,128)(2,1)} %bitcast.12, bf16[144,768]{1,0:T(8,128)(2,1)} %bitcast.13, bf16[144,1536]{1,0:T(8,128)(2,1)} %bitcast.7, ...), custom_call_target="tpu_custom_call" | custom-call | tf_op jit(solution)/shard_map/pallas_call | solution.py:383
  47.1 1.6 %copy.14 = bf16[1,1,1,1,144,768]{5,4,3,2,1,0:T(8,128)(2,1)} copy(bf16[1,1,1,1,144,768]{5,4,3,2,1,0:T(8,128)(2,1)} %bitcast.10) | data formatting | bytes 442368
  48.7 1.6 %copy.15 = bf16[1,1,1,1,144,768]{5,4,3,2,1,0:T(8,128)(2,1)} copy(bf16[1,1,1,1,144,768]{5,4,3,2,1,0:T(8,128)(2,1)} %bitcast.9) | data formatting | bytes 442368
  50.4 1.6 %copy.16 = bf16[1,1,1,1,144,768]{5,4,3,2,1,0:T(8,128)(2,1)} copy(bf16[1,1,1,1,144,768]{5,4,3,2,1,0:T(8,128)(2,1)} %bitcast.8) | data formatting | bytes 442368
  52.0 1.6 %copy.17 = f32[48,768]{1,0:T(8,128)} copy(f32[48,768]{1,0:T(8,128)} %get-tuple-element.19) | data formatting | bytes 294912

commit v2 on v1

--- a/solution.py
+++ b/solution.py
@@ -18,10 +18,18 @@
     return lax.dot_general(a, b, (dims, ((), ())), preferred_element_type=F32)
 
 
+def lone_head(heads, reach_ref):
+    alone = jnp.int32(0)
+    for n in reversed(range(heads)):
+        reach = reach_ref[n, 2] + reach_ref[n, 3] + reach_ref[n, 4] + reach_ref[n, 5]
+        alone = jnp.where(reach == 0, n, alone)
+    return alone
+
+
 def kernel(
-    sizes, heads, q_ref, k_ref, v_ref, og_ref, w_ref, reach_ref, gq_ref, gk_ref, gv_ref, gw_ref,
+    sizes, heads, q_ref, k_ref, v_ref, og_any, w_any, reach_ref, dq_sl, dk_sl, dw_sl,
     kv, q_sl, da_sl, og_s, og_g, og_t, att, s_ref, dp_ref, p_low, ds_low,
-    back_out, back_in, side_out, side_in, acc, dk_sl, dq_sl, dw_out, dw_in, dw_sl,
+    back_out, back_in, side_out, side_in, acc, dw_out, dw_in, og_ref, w_ref, in_sem,
     w_send, w_recv, h_send, h_recv, bh_send, bh_recv, bw_send, bw_recv,
     og_send, og_recv, at_send, at_recv, dw_send, dw_recv,
 ):
@@ -30,7 +38,7 @@
     tile = q_ref.shape[0]
     model = og_ref.shape[1]
     quarter = model // 4
-    block = gw_ref.shape[0]
+    block = dw_sl.shape[1]
     run = n_wa * block
     scale = 1.0 / math.sqrt(HD)
     dp, ha, wa = (lax.axis_index(a) for a in ("dp", "ha", "wa"))
@@ -100,6 +108,10 @@
             dw_recv.at[step - 1, i], device,
         )
 
+    og_in = pltpu.make_async_copy(og_any, og_ref, in_sem.at[0])
+    w_in = pltpu.make_async_copy(w_any, w_ref, in_sem.at[1])
+    og_in.start()
+    w_in.start()
     barrier = pltpu.get_barrier_semaphore()
 
     def greet(device):
@@ -114,10 +126,7 @@
     for step in range(1, peers):
         greet(peer_at(step)[1])
 
-    alone = jnp.int32(0)
-    for n in reversed(range(heads)):
-        reach = reach_ref[n, 2] + reach_ref[n, 3] + reach_ref[n, 4] + reach_ref[n, 5]
-        alone = jnp.where(reach == 0, n, alone)
+    alone = lone_head(heads, reach_ref)
 
     def pick(i, read):
         if i < sent:
@@ -127,25 +136,12 @@
             value = jnp.where(alone == n, read(n), value)
         return value
 
-    def place(n, read):
-        value = read(sent)
-        if n < sent:
-            value = jnp.where(alone > n, read(n), value)
-        if n > 0:
-            value = jnp.where(alone < n, read(n - 1), value)
-        return value
-
     def columns(ref):
         return lambda n: ref[:, n * HD : (n + 1) * HD]
 
     for i in range(sent):
         kv[i, 4, :, :HD] = pick(i, columns(k_ref))
         kv[i, 4, :, HD:] = pick(i, columns(v_ref))
-    for m in range(4):
-        for r in range(runs):
-            first = (r // (n_ha // 2) * 2 + m // 2) * n_ha + (r % (n_ha // 2)) * 2 + m % 2
-            og_s[m, :, r * run : (r + 1) * run] = og_ref[:, first * run : (first + 1) * run]
-
     for d in range(2):
         @pl.when(jnp.logical_not(wide[d][0]))
         def _():
@@ -173,8 +169,14 @@
             @pl.when(high[d][0])
             def _():
                 h_copy(d, 1, i).start()
+    og_in.wait()
+    for m in range(4):
+        for r in range(runs):
+            first = (r // (n_ha // 2) * 2 + m // 2) * n_ha + (r % (n_ha // 2)) * 2 + m % 2
+            og_s[m, :, r * run : (r + 1) * run] = og_ref[:, first * run : (first + 1) * run]
     for j in range(1, 4):
         og_copy(j).start()
+    w_in.wait()
 
     grad_attn = dot(og_ref[...], w_ref[...], ((1,), (0,))).astype(BF)
     for i in range(heads):
@@ -321,9 +323,6 @@
     if sent > 1:
         fold_wide(sent - 2)
 
-    for n in range(heads):
-        gq_ref[:, n * HD : (n + 1) * HD] = place(n, lambda i: dq_sl[i])
-
     def gather_w(i, carry):
         total = dw_out[i, my_peer].astype(F32)
         for b in range(1, peers):
@@ -334,12 +333,6 @@
 
     lax.fori_loop(0, heads, gather_w, 0)
     fold_wide(sent - 1)
-    for n in range(heads):
-        at = slice(n * HD, (n + 1) * HD)
-        gk_ref[:, at] = place(n, lambda i: dk_sl[i, :, :HD])
-        gv_ref[:, at] = place(n, lambda i: dk_sl[i, :, HD:])
-        gw_ref[:, at] = place(n, lambda i: dw_sl[i])
-
     def drain(i, carry):
         for d in range(2):
             @pl.when(wide[d][0])
@@ -366,6 +359,17 @@
     lax.fori_loop(0, heads, drain_w, 0)
     for j in range(1, 4):
         og_copy(j).wait_send()
+
+
+def in_head_order(heads, reach_ref, dq_sl, dk_sl, dw_sl, gq_ref, gk_ref, gv_ref, gw_ref):
+    alone = lone_head(heads, reach_ref)
+    for n in range(heads):
+        slot = jnp.where(alone == n, heads - 1, n - jnp.where(alone < n, 1, 0))
+        at = slice(n * HD, (n + 1) * HD)
+        gq_ref[:, at] = dq_sl[slot]
+        gk_ref[:, at] = dk_sl[slot, :, :HD]
+        gv_ref[:, at] = dk_sl[slot, :, HD:]
+        gw_ref[:, at] = dw_sl[slot]
 
 
 def shards(sizes, queries, key_tiles, value_tiles, out_grad, w_out, reaches):
@@ -379,12 +383,17 @@
     rows = [a.reshape(a.shape[-2:]) for a in (queries, key_tiles, value_tiles, out_grad)]
     sem = pltpu.SemaphoreType.DMA
     vmem = pl.BlockSpec(memory_space=pltpu.VMEM)
+    smem = pl.BlockSpec(memory_space=pltpu.SMEM)
     grads = jax.ShapeDtypeStruct((tile, width), BF)
-    out = pl.pallas_call(
+    slots = pl.pallas_call(
         functools.partial(kernel, sizes, heads),
-        out_shape=(grads, grads, grads, jax.ShapeDtypeStruct((block, width), F32)),
-        in_specs=[vmem] * 5 + [pl.BlockSpec(memory_space=pltpu.SMEM)],
-        out_specs=(vmem,) * 4,
+        out_shape=(
+            jax.ShapeDtypeStruct((heads, tile, HD), BF),
+            jax.ShapeDtypeStruct((heads, tile, 2 * HD), BF),
+            jax.ShapeDtypeStruct((heads, block, HD), F32),
+        ),
+        in_specs=[vmem] * 3 + [pl.BlockSpec(memory_space=pl.ANY)] * 2 + [smem],
+        out_specs=(vmem,) * 3,
         scratch_shapes=[
             pltpu.VMEM((sent, 9, tile, 2 * HD), BF),
             pltpu.VMEM((heads, tile, HD), BF),
@@ -402,11 +411,11 @@
             pltpu.VMEM((sent, 2, tile, 2 * HD), BF),
             pltpu.VMEM((sent, 2, tile, 2 * HD), BF),
             pltpu.VMEM((sent, 3, tile, 2 * HD), F32),
-            pltpu.VMEM((heads, tile, 2 * HD), BF),
-            pltpu.VMEM((heads, tile, HD), BF),
             pltpu.VMEM((heads, peers, block, HD), BF),
             pltpu.VMEM((heads, peers - 1, block, HD), BF),
-            pltpu.VMEM((heads, block, HD), F32),
+            pltpu.VMEM((tile, model), BF),
+            pltpu.VMEM((model, width), BF),
+            sem((2,)),
             sem((2, sent)), sem((2, sent)), sem((2, 3, sent)), sem((2, 3, sent)),
             sem((2, sent)), sem((2, sent)), sem((2, sent)), sem((2, sent)),
             sem((3,)), sem((3,)), sem((3, heads)), sem((3, heads)),
@@ -416,6 +425,12 @@
             collective_id=0, has_side_effects=True, vmem_limit_bytes=60 * 1024 * 1024
         ),
     )(*rows, w_out, reaches)
+    out = pl.pallas_call(
+        functools.partial(in_head_order, heads),
+        out_shape=(grads, grads, grads, jax.ShapeDtypeStruct((block, width), F32)),
+        in_specs=[smem] + [vmem] * 3,
+        out_specs=(vmem,) * 4,
+    )(reaches, *slots)
     return tuple(o.reshape(queries.shape) for o in out[:3]) + (out[3],)
 
 

time: 54.2 us -> 48.9 us (0.902)
  local copies, waits for them, and re-layouts: 6.48 us -> 0 us
  Pallas kernels: 46.5 us -> 47.8 us
    unnamed x4 -> x0, local copies, waits for them, and re-layouts: 6.48 us -> none
    pallas_call x1 -> x2, Pallas kernels: 46.5 us -> 47.8 us  [the longest x1 45.6 us: shards(): pl.pallas_call(functools.partial(kernel, sizes, heads), out_shape=(jax.Sh...]
where the time goes in v2:
time: 48.9 us; the launch traced here: 48.4 us
  Pallas kernels  47.8 us (98%)
  between operations  0.64 us (1%)
    pallas_call x1, Pallas kernels, shards(): pl.pallas_call(functools.partial(kernel, sizes, heads), out_shape=(jax.Sh...  45.6 us
    pallas_call x1, Pallas kernels, shards(): pl.pallas_call(functools.partial(in_head_order, heads), out_shape=(grads,...  2.19 us

profile of v2, /device:TPU:0, one launch (start us, length us, event | category | flops | bytes accessed | tf_op | source)
XLA Modules:
  0.0 48.4 jit_solution(3110863403113025447)
XLA Ops:
  0.6 45.6 %shard_map.93 = (bf16[6,144,128]{2,1,0:T(8,128)(2,1)}, bf16[6,144,256]{2,1,0:T(8,128)(2,1)}, f32[6,48,128]{2,1,0:T(8,128)}) custom-call(bf16[144,768]{1,0:T(8,128)(2,1)} %bitcast.8, bf16[144,768]{1,0:T(8,128)(2,1)} %bitcast.9, bf16[144,768]{1,0:T(8,128)(2,1)} %bitcast.10, bf16[144,1536]{1,0:T(8,128)(2,1)} %bitcast.7, bf16[1536,768]{1,0:T(8,128)(2,1)} %w_any.1, ...), custom_call_target="tpu_custom_call" | custom-call | tf_op jit(solution)/shard_map/pallas_call | solution.py:388
  46.2 2.2 %shard_map.94 = (bf16[144,768]{1,0:T(8,128)(2,1)}, bf16[144,768]{1,0:T(8,128)(2,1)}, bf16[144,768]{1,0:T(8,128)(2,1)}, f32[48,768]{1,0:T(8,128)}) custom-call(s32[6,6]{1,0:T(8,128)} %reach_ref.3, bf16[6,144,128]{2,1,0:T(8,128)(2,1)} %get-tuple-element.11.dq_sl, bf16[6,144,256]{2,1,0:T(8,128)(2,1)} %get-tuple-element.12.dk_sl, ...), custom_call_target="tpu_custom_call" | custom-call | tf_op jit(solution)/shard_map/pallas_call | solution.py:428

commit v3 on v2

--- a/solution.py
+++ b/solution.py
@@ -29,9 +29,9 @@
 def kernel(
     sizes, heads, q_ref, k_ref, v_ref, og_any, w_any, reach_ref, dq_sl, dk_sl, dw_sl,
     kv, q_sl, da_sl, og_s, og_g, og_t, att, s_ref, dp_ref, p_low, ds_low,
-    back_out, back_in, side_out, side_in, acc, dw_out, dw_in, og_ref, w_ref, in_sem,
+    back_out, back_in, side_out, side_in, acc, dw_out, dw_in, dz_out, dz_in, og_ref, w_ref, in_sem,
     w_send, w_recv, h_send, h_recv, bh_send, bh_recv, bw_send, bw_recv,
-    og_send, og_recv, at_send, at_recv, dw_send, dw_recv,
+    og_send, og_recv, at_send, at_recv, dw_send, dw_recv, dz_send, dz_recv, x_send, x_recv,
 ):
     n_dp, n_ha, n_wa = sizes
     sent = heads - 1
@@ -53,16 +53,15 @@
         group.append((d_lo * 2 + h_lo, (dp_hi * 2 + d_lo, ha_hi * 2 + h_lo, wa)))
     runs = (n_dp // 2) * (n_ha // 2)
     peers = runs * n_wa
-    my_peer = (dp_hi * (n_ha // 2) + ha_hi) * n_wa + wa
-
-    def peer_at(step):
-        at = lax.rem(my_peer + step, peers)
-        r = at // n_wa
-        return at, (
-            (r // (n_ha // 2)) * 2 + dp_lo,
-            (r % (n_ha // 2)) * 2 + ha_lo,
-            at % n_wa,
-        )
+    my_run = dp_hi * (n_ha // 2) + ha_hi
+
+    def run_at(step):
+        r = lax.rem(my_run + step, runs)
+        return r, ((r // (n_ha // 2)) * 2 + dp_lo, (r % (n_ha // 2)) * 2 + ha_lo, wa)
+
+    def column_at(step):
+        at = lax.rem(wa + step, n_wa)
+        return at, (dp, ha, at)
 
     def remote(src, dst, s, r, device):
         return pltpu.make_async_remote_copy(
@@ -102,11 +101,27 @@
         )
 
     def dw_copy(step, i):
-        at, device = peer_at(step)
-        return remote(
-            dw_out.at[i, at], dw_in.at[i, step - 1], dw_send.at[step - 1, i],
+        r, device = run_at(step)
+        return remote(
+            dw_out.at[i, r], dw_in.at[i, step - 1], dw_send.at[step - 1, i],
             dw_recv.at[step - 1, i], device,
         )
+
+    def dz_copy(step, i):
+        at, device = column_at(step)
+        return remote(
+            dz_out.at[i, at], dz_in.at[i, step - 1], dz_send.at[step - 1, i],
+            dz_recv.at[step - 1, i], device,
+        )
+
+    def x_copy(d, e, i):
+        return remote(
+            kv.at[i, 6 * d + 1], kv.at[i, 6 * d + 2 * (1 - e)], x_send.at[d, e, i],
+            x_recv.at[d, e, i], wide[e][1],
+        )
+
+    def crosses(d, i):
+        return (i % 2 == 1) & (ha_lo == d)
 
     og_in = pltpu.make_async_copy(og_any, og_ref, in_sem.at[0])
     w_in = pltpu.make_async_copy(w_any, w_ref, in_sem.at[1])
@@ -123,8 +138,10 @@
         pl.when(exists)(functools.partial(greet, device))
     for _, device in group:
         greet(device)
-    for step in range(1, peers):
-        greet(peer_at(step)[1])
+    for step in range(1, runs):
+        greet(run_at(step)[1])
+    for step in range(1, n_wa):
+        greet(column_at(step)[1])
 
     alone = lone_head(heads, reach_ref)
 
@@ -148,6 +165,11 @@
             for i in range(sent):
                 kv[i, 3 + 2 * d] = jnp.zeros((tile, 2 * HD), BF)
                 side_in[i, 1 - d] = jnp.zeros((tile, 2 * HD), BF)
+            for h in range(2):
+                @pl.when(high[h][0] & (ha_lo == h))
+                def _():
+                    for i in range(1, sent, 2):
+                        kv[i, 6 * h + 2 * d] = jnp.zeros((tile, 2 * HD), BF)
 
         @pl.when(jnp.logical_not(high[d][0]))
         def _():
@@ -155,7 +177,7 @@
                 kv[i, 6 * d : 6 * d + 3] = jnp.zeros((3, tile, 2 * HD), BF)
                 back_in[i, 1 - d] = jnp.zeros((3, tile, 2 * HD), BF)
 
-    waits = 3 + peers - 1
+    waits = 3 + runs - 1 + n_wa - 1
     for exists, _ in wide + high:
         waits = waits + jnp.where(exists, 1, 0)
     pl.semaphore_wait(barrier, waits)
@@ -222,10 +244,16 @@
             def _():
                 w_copy(d, i).wait_recv()
         for d in range(2):
-            @pl.when(high[d][0])
+            @pl.when(high[d][0] & jnp.logical_not(crosses(d, i)))
             def _():
                 h_copy(d, 0, i).start()
                 h_copy(d, 2, i).start()
+        for d in range(2):
+            @pl.when(high[d][0] & crosses(d, i))
+            def _():
+                h_copy(1 - d, 1, i).wait_recv()
+                for e in range(2):
+                    pl.when(wide[e][0])(lambda: x_copy(d, e, i).start())
 
     def fold_high(i):
         for d in range(2):
@@ -257,9 +285,19 @@
             at_copy(j, i).wait_recv()
         part = dot(og_t[...], att[i].reshape(4 * tile, HD), ((1,), (0,)))
         for b in range(peers):
-            dw_out[i, b] = part[b * block : (b + 1) * block].astype(BF)
-        for b in range(1, peers):
+            rows = part[b * block : (b + 1) * block]
+            dw_out[i, b // n_wa, b % n_wa] = rows.astype(BF)
+        for b in range(1, runs):
             dw_copy(b, i).start()
+
+    def pass_on(i):
+        total = dw_out[i, my_run].astype(F32)
+        for b in range(1, runs):
+            dw_copy(b, i).wait_recv()
+            total = total + dw_in[i, b - 1].astype(F32)
+        dz_out[i] = total.astype(BF)
+        for b in range(1, n_wa):
+            dz_copy(b, i).start()
 
     def window(i):
         def reach(c):
@@ -288,10 +326,15 @@
     def step(i, carry):
         pl.when(i + 2 < sent)(lambda: relay(i + 2))
         for d in range(2):
-            @pl.when(high[1 - d][0])
+            @pl.when(high[1 - d][0] & jnp.logical_not(crosses(1 - d, i)))
             def _():
                 for c in range(3):
                     h_copy(d, c, i).wait_recv()
+
+            @pl.when(high[1 - d][0] & crosses(1 - d, i))
+            def _():
+                for e in range(2):
+                    pl.when(wide[1 - e][0])(lambda: x_copy(1 - d, e, i).wait_recv())
         near = kv[i].reshape(9 * tile, 2 * HD)
         dk, dv = attend(
             i, q_sl[i], da_sl[i], near[:, :HD], near[:, HD:], 9 * tile, window(i)
@@ -314,20 +357,28 @@
         def _():
             project(i - 1)
             fold_high(i - 1)
-        pl.when(i >= 2)(lambda: fold_wide(i - 2))
+
+        pl.when(i == 0)(lambda: pass_on(sent))
+
+        @pl.when(i >= 2)
+        def _():
+            pass_on(i - 2)
+            fold_wide(i - 2)
+
         return carry
 
     lax.fori_loop(0, sent, step, 0)
     project(sent - 1)
     fold_high(sent - 1)
-    if sent > 1:
-        fold_wide(sent - 2)
+    pass_on(sent - 2)
+    fold_wide(sent - 2)
+    pass_on(sent - 1)
 
     def gather_w(i, carry):
-        total = dw_out[i, my_peer].astype(F32)
-        for b in range(1, peers):
-            dw_copy(b, i).wait_recv()
-            total = total + dw_in[i, b - 1].astype(F32)
+        total = dz_out[i, wa].astype(F32)
+        for b in range(1, n_wa):
+            dz_copy(b, i).wait_recv()
+            total = total + dz_in[i, b - 1].astype(F32)
         dw_sl[i] = total
         return carry
 
@@ -342,9 +393,18 @@
 
             @pl.when(high[d][0])
             def _():
-                for c in range(3):
-                    h_copy(d, c, i).wait_send()
+                h_copy(d, 1, i).wait_send()
                 bh_copy(d, i).wait_send()
+
+            @pl.when(high[d][0] & jnp.logical_not(crosses(d, i)))
+            def _():
+                h_copy(d, 0, i).wait_send()
+                h_copy(d, 2, i).wait_send()
+
+            @pl.when(high[d][0] & crosses(d, i))
+            def _():
+                for e in range(2):
+                    pl.when(wide[e][0])(lambda: x_copy(d, e, i).wait_send())
         return carry
 
     lax.fori_loop(0, sent, drain, 0)
@@ -352,8 +412,10 @@
     def drain_w(i, carry):
         for j in range(1, 4):
             at_copy(j, i).wait_send()
-        for b in range(1, peers):
+        for b in range(1, runs):
             dw_copy(b, i).wait_send()
+        for b in range(1, n_wa):
+            dz_copy(b, i).wait_send()
         return carry
 
     lax.fori_loop(0, heads, drain_w, 0)
@@ -379,7 +441,8 @@
     sent = heads - 1
     devices = sizes[0] * sizes[1] * sizes[2]
     block = model // devices
-    peers = devices // 4
+    columns = sizes[2]
+    runs = devices // 4 // columns
     rows = [a.reshape(a.shape[-2:]) for a in (queries, key_tiles, value_tiles, out_grad)]
     sem = pltpu.SemaphoreType.DMA
     vmem = pl.BlockSpec(memory_space=pltpu.VMEM)
@@ -411,15 +474,19 @@
             pltpu.VMEM((sent, 2, tile, 2 * HD), BF),
             pltpu.VMEM((sent, 2, tile, 2 * HD), BF),
             pltpu.VMEM((sent, 3, tile, 2 * HD), F32),
-            pltpu.VMEM((heads, peers, block, HD), BF),
-            pltpu.VMEM((heads, peers - 1, block, HD), BF),
+            pltpu.VMEM((heads, runs, columns, block, HD), BF),
+            pltpu.VMEM((heads, runs - 1, columns, block, HD), BF),
+            pltpu.VMEM((heads, columns, block, HD), BF),
+            pltpu.VMEM((heads, columns - 1, block, HD), BF),
             pltpu.VMEM((tile, model), BF),
             pltpu.VMEM((model, width), BF),
             sem((2,)),
             sem((2, sent)), sem((2, sent)), sem((2, 3, sent)), sem((2, 3, sent)),
             sem((2, sent)), sem((2, sent)), sem((2, sent)), sem((2, sent)),
             sem((3,)), sem((3,)), sem((3, heads)), sem((3, heads)),
-            sem((peers - 1, heads)), sem((peers - 1, heads)),
+            sem((runs - 1, heads)), sem((runs - 1, heads)),
+            sem((columns - 1, heads)), sem((columns - 1, heads)),
+            sem((2, 2, sent)), sem((2, 2, sent)),
         ],
         compiler_params=pltpu.CompilerParams(
             collective_id=0, has_side_effects=True, vmem_limit_bytes=60 * 1024 * 1024

time: 48.9 us -> 48.6 us (level)
  no operation moved by 1% of the time
where the time goes in v3:
time: 48.6 us; the launch traced here: 48.4 us
  Pallas kernels  47.8 us (98%)
  between operations  0.64 us (1%)
    pallas_call x1, Pallas kernels, shards(): pl.pallas_call(functools.partial(kernel, sizes, heads), out_shape=(jax.Sh...  45.6 us
    pallas_call x1, Pallas kernels, shards(): pl.pallas_call(functools.partial(in_head_order, heads), out_shape=(grads,...  2.19 us

profile of v3, /device:TPU:0, one launch (start us, length us, event | category | flops | bytes accessed | tf_op | source)
XLA Modules:
  0.0 48.4 jit_solution(4790921400195797441)
XLA Ops:
  0.6 45.6 %shard_map.93 = (bf16[6,144,128]{2,1,0:T(8,128)(2,1)}, bf16[6,144,256]{2,1,0:T(8,128)(2,1)}, f32[6,48,128]{2,1,0:T(8,128)}) custom-call(bf16[144,768]{1,0:T(8,128)(2,1)} %bitcast.8, bf16[144,768]{1,0:T(8,128)(2,1)} %bitcast.9, bf16[144,768]{1,0:T(8,128)(2,1)} %bitcast.10, bf16[144,1536]{1,0:T(8,128)(2,1)} %bitcast.7, bf16[1536,768]{1,0:T(8,128)(2,1)} %w_any.1, ...), custom_call_target="tpu_custom_call" | custom-call | tf_op jit(solution)/shard_map/pallas_call | solution.py:451
  46.3 2.2 %shard_map.94 = (bf16[144,768]{1,0:T(8,128)(2,1)}, bf16[144,768]{1,0:T(8,128)(2,1)}, bf16[144,768]{1,0:T(8,128)(2,1)}, f32[48,768]{1,0:T(8,128)}) custom-call(s32[6,6]{1,0:T(8,128)} %reach_ref.3, bf16[6,144,128]{2,1,0:T(8,128)(2,1)} %get-tuple-element.11.dq_sl, bf16[6,144,256]{2,1,0:T(8,128)(2,1)} %get-tuple-element.12.dk_sl, ...), custom_call_target="tpu_custom_call" | custom-call | tf_op jit(solution)/shard_map/pallas_call | solution.py:495
